TPU v7x, 256 devices: a whole 4x4x8 slice. The times are simulated.
256 devices in a mesh: ctg: 32 (over x, y, core), br: 8 (over z).
Axes of the slice: x: 4, y: 4, z: 8, core: 2. Of those that a mesh axis runs over, the one named last changes fastest.
Arguments:
- base_vm: float32 [10240], P(('ctg', 'br')), may hold values from 0.95 to 1.05
- base_va: float32 [10240], P(('ctg', 'br')), may hold values from -0.6 to 0.6
- delta_state: float32 [256, 2, 10240], P('ctg', None, 'br'), may hold values from -0.18 to 0.18
- multipliers: float32 [256, 2, 10240], P('ctg', None, 'br'), may hold values from -6 to 6
- net_inj: float32 [256, 2, 10240], P('ctg', None, 'br'), may hold values from -6 to 6
- ang_grad: float32 [256, 10240], P('ctg', 'br'), may hold values from -6 to 6
- from_bus: int32 [13312], P('br'), may hold values from 0 to 10239
- to_bus: int32 [13312], P('br'), may hold values from 0 to 10239
- status: int32 [256, 13312], P('ctg', 'br'), may hold values 0 or 1
- conduct: float32 [13312], P('br'), may hold values from 1 to 5
- suscept: float32 [13312], P('br'), may hold values from -15 to -5
- charging: float32 [13312], P('br'), may hold values from 0.1 to 0.6
- rating: float32 [13312], P('br'), may hold values from 1 to 3
- slack: float32 [256, 13312], P('ctg', 'br'), may hold values from 0.05 to 2
- zdual: float32 [256, 13312], P('ctg', 'br'), may hold values from 0.05 to 2
Outputs:
- mismatch: float32 [256, 2, 10240], P('ctg', None, 'br')
- dual_res: float32 [256, 10240], P('ctg', 'br')
- limit_res: float32 [256, 13312], P('ctg', 'br')
- ctg_norms: float32 [256, 4], P('ctg')
- total_norms: float32 [4], replicated
All inputs are finite; a program needn't handle non-finite values. No bound on the sum of `status` on one device may be relied on, other than what follows from the above.
Results may differ from a plain program's by a relative error of at most 0.0003.
Values sent between devices are 32-bit elements; how exact they have to be, the bound alone decides.
A program may use at most 64 MiB of HBM per device.

v0:
```python
import math
import jax
import jax.numpy as jnp
from jax import lax
from jax.sharding import PartitionSpec as P


def turned_gather(arrays, axis, dims):
    turned = [jnp.moveaxis(a, dim, 0) for a, dim in zip(arrays, dims)]
    widths = [t[0].size for t in turned]
    both = jnp.concatenate([t.reshape(-1, w) for t, w in zip(turned, widths)], axis=1)
    whole = lax.all_gather(both, axis, axis=0, tiled=True)
    pieces = jnp.split(whole, [sum(widths[:k]) for k in range(1, len(widths))], axis=1)
    return tuple(
        (
            jnp.moveaxis(b.reshape(-1, *t.shape[1:]), 0, dim)
            for b, t, dim in zip(pieces, turned, dims)
        )
    )


def in_one_piece(arrays, axis, dim, along):
    both = jnp.concatenate(arrays, axis=along)
    whole, at, finished = (lax.all_gather(both, axis, axis=dim, tiled=True), 0, [])
    for a in arrays:
        finished.append(lax.slice_in_dim(whole, at, at + a.shape[along], axis=along))
        at += a.shape[along]
    return tuple(finished)


def in_blocks(array, dim, peers):
    shape = array.shape
    pieces = array.reshape(*shape[:dim], peers, shape[dim] // peers, *shape[dim + 1 :])
    return jnp.moveaxis(pieces, dim, 0)


def summed_on_arrival(array, axis, dim):
    peers = lax.axis_size(axis)
    pieces = lax.all_to_all(in_blocks(array, dim, peers), axis, 0, 0, tiled=True)
    return jnp.sum(pieces, axis=0)


def sent_to_all(array, axis):
    copies = jnp.broadcast_to(array, (lax.axis_size(axis), *array.shape))
    return lax.all_to_all(copies, axis, split_axis=0, concat_axis=0, tiled=True)


def over_copies(array, axis):
    everything = sent_to_all(array, axis)
    return jnp.sum(everything, axis=0)


def in_one(arrays, axis):
    ends = [0]
    for a in arrays:
        ends.append(ends[-1] + a.size)
    subtotal = over_copies(jnp.concatenate([a.ravel() for a in arrays]), axis)
    return tuple((subtotal[b:e].reshape(a.shape) for a, b, e in zip(arrays, ends, ends[1:])))


def block_size(span_total, other_side):
    limit = max(128, (1 << 23) // other_side)
    power = 1 << limit.bit_length() - 1
    return math.gcd(span_total, min(1024, power))


def select_cols(values, index_list):
    row_count, bus_count = values.shape
    col_count = index_list.shape[0]
    span_cols = block_size(bus_count, col_count)
    block_count = bus_count // span_cols
    tiles = values.reshape(row_count, block_count, span_cols).transpose(1, 0, 2)

    def add_block(running, item):
        segment, number = item
        labels = number * span_cols + lax.iota(jnp.int32, span_cols)
        onehot = (labels[:, None] == index_list[None, :]).astype(jnp.float32)
        running = running + jnp.dot(
            segment, onehot, precision=lax.Precision.HIGHEST, preferred_element_type=jnp.float32
        )
        return (running, None)

    start_zero = jnp.zeros((row_count, col_count), jnp.float32)
    numbers = jnp.arange(block_count, dtype=jnp.int32)
    result, _ = lax.scan(add_block, start_zero, (tiles, numbers))
    return result


def spread_rows(values, index_list, bus_count):
    row_count, col_count = values.shape
    span_cols = block_size(bus_count, col_count)
    block_count = bus_count // span_cols

    def one_block(carry, number):
        labels = number * span_cols + lax.iota(jnp.int32, span_cols)
        onehot = (index_list[:, None] == labels[None, :]).astype(jnp.float32)
        piece_sum = jnp.dot(
            values, onehot, precision=lax.Precision.HIGHEST, preferred_element_type=jnp.float32
        )
        return (carry, piece_sum)

    numbers = jnp.arange(block_count, dtype=jnp.int32)
    _, pieces = lax.scan(one_block, jnp.int32(0), numbers)
    return pieces.transpose(1, 0, 2).reshape(row_count, bus_count)


def branch_flows(
    volt_mag, volt_ang, mult_p, mult_q, from_idx, to_idx, conduct, suscept, charging, in_service
):
    scen_count = volt_mag.shape[0]
    stacked = jnp.concatenate([volt_mag, volt_ang, mult_p, mult_q], 0)
    at_from_end = select_cols(stacked, from_idx)
    at_to_end = select_cols(stacked, to_idx)
    volt_from = at_from_end[:scen_count]
    volt_to = at_to_end[:scen_count]
    angle_diff = at_from_end[scen_count : 2 * scen_count] - at_to_end[scen_count : 2 * scen_count]
    mp_from = at_from_end[2 * scen_count : 3 * scen_count]
    mq_from = at_from_end[3 * scen_count :]
    mp_to = at_to_end[2 * scen_count : 3 * scen_count]
    mq_to = at_to_end[3 * scen_count :]
    cos_diff = jnp.cos(angle_diff)
    sin_diff = jnp.sin(angle_diff)
    volt_prod = volt_from * volt_to
    p_from = conduct * volt_from * volt_from - volt_prod * (conduct * cos_diff + suscept * sin_diff)
    q_from = -(suscept + charging) * volt_from * volt_from - volt_prod * (
        conduct * sin_diff - suscept * cos_diff
    )
    p_to = conduct * volt_to * volt_to - volt_prod * (conduct * cos_diff - suscept * sin_diff)
    q_to = -(suscept + charging) * volt_to * volt_to + volt_prod * (
        conduct * sin_diff + suscept * cos_diff
    )
    flow_dual = volt_prod * (
        mp_from * (conduct * sin_diff - suscept * cos_diff)
        - mq_from * (conduct * cos_diff + suscept * sin_diff)
        + mp_to * (conduct * sin_diff + suscept * cos_diff)
        + mq_to * (conduct * cos_diff - suscept * sin_diff)
    )
    at_from = jnp.stack([p_from, q_from, flow_dual], 1) * in_service[:, None, :]
    at_to = jnp.stack([p_to, q_to, -flow_dual], 1) * in_service[:, None, :]
    return (at_from, at_to)


def sum_at_buses(from_vals, to_vals, from_idx, to_idx, offset, bus_count):
    scen_count = from_vals.shape[0]
    both_vals = jnp.concatenate([from_vals, to_vals], 2).reshape(scen_count * 3, -1)
    both_idx = jnp.concatenate([from_idx, to_idx], 0) - offset
    summed = spread_rows(both_vals, both_idx, bus_count)
    return summed.reshape(scen_count, 3, bus_count)


def per_device(
    base_vm,
    base_va,
    delta_state,
    multipliers,
    net_inj,
    ang_grad,
    from_bus,
    to_bus,
    status,
    conduct,
    suscept,
    charging,
    rating,
    slack,
    zdual,
):
    full_vm, full_va = turned_gather((base_vm, base_va), ("ctg", "br"), (0, 0))
    shifts, duals_all = in_one_piece((delta_state, multipliers), "br", 2, 0)
    volt_mag = full_vm[None, :] + shifts[:, 0]
    volt_ang = full_va[None, :] + shifts[:, 1]
    in_service = status.astype(jnp.float32)
    at_from, at_to = branch_flows(
        volt_mag,
        volt_ang,
        duals_all[:, 0],
        duals_all[:, 1],
        from_bus,
        to_bus,
        conduct,
        suscept,
        charging,
        in_service,
    )
    limit_res = in_service * (
        at_from[:, 0] * at_from[:, 0] + at_from[:, 1] * at_from[:, 1] + slack - rating * rating
    )
    complement = in_service * (zdual * slack - 0.01)
    limit_part = jnp.sum(limit_res * limit_res, axis=1)
    comp_part = jnp.sum(complement * complement, axis=1)
    bus_terms = sum_at_buses(at_from, at_to, from_bus, to_bus, 0, shifts.shape[2])
    summed = summed_on_arrival(bus_terms, "br", 2)
    mismatch = summed[:, :2] - net_inj
    dual_res = summed[:, 2] + ang_grad
    mis_part = jnp.sum(mismatch * mismatch, axis=(1, 2))
    dual_part = jnp.sum(dual_res * dual_res, axis=1)
    mis_sq, dual_sq, limit_sq, comp_sq = in_one((mis_part, dual_part, limit_part, comp_part), "br")
    squares = jnp.stack([mis_sq, dual_sq, limit_sq, comp_sq], 1)
    ctg_norms = jnp.sqrt(squares)
    totals = over_copies(jnp.sum(squares, axis=0), "ctg")
    total_norms = jnp.sqrt(totals / (delta_state.shape[0] * lax.axis_size("ctg")))
    return (mismatch, dual_res, limit_res, ctg_norms, total_norms)


def solution(mesh):
    placed = (
        P(("ctg", "br")),
        P(("ctg", "br")),
        P("ctg", None, "br"),
        P("ctg", None, "br"),
        P("ctg", None, "br"),
        P("ctg", "br"),
        P("br"),
        P("br"),
        P("ctg", "br"),
        P("br"),
        P("br"),
        P("br"),
        P("br"),
        P("ctg", "br"),
        P("ctg", "br"),
    )
    return jax.shard_map(
        per_device,
        mesh=mesh,
        in_specs=placed,
        out_specs=(P("ctg", None, "br"), P("ctg", "br"), P("ctg", "br"), P("ctg", None), P()),
        check_vma=False,
    )
```

profile of v0, /device:TPU:1, one launch (start us, length us, event | category | flops | bytes accessed | tf_op | source)
XLA Modules:
  0.0 281.0 jit_solution(867481893369995764)
XLA Ops:
  10.5 67.2 %all-gather = f32[256,40,2]{1,2,0:T(2,128)S(1)} all-gather(f32[1,40,2]{1,2,0:T(2,128)S(1)} %maximum_bitcast_fusion.1), channel_id=1, replica_groups=mesh['ctg'=32,'br'=8] {'ctg','br'}, dimensions={0}, use_global_device_ids=true | all-gather | bytes 82240 | tf_op jit(solution)/shard_map/all_gather | solution.py:12
  79.9 36.7 %while.34 = (s32[]{:T(128)}, f32[32,1664]{1,0:T(8,128)S(1)}, f32[10,32,1024]{2,1,0:T(8,128)S(1)}, s32[10]{0:T(128)S(1)}, s32[1664]{0:T(1024)S(1)}, /*index=5*/s32[]{:T(128)}, s32[1]{0:T(128)}, s32[]{:T(128)}) while((s32[]{:T(128)}, f32[32,1664]{1,0:T(8,128)S(1)}, f32[10,32,1024]{2,1,0:T(8,128)S(1)}, s32[10]{0:T(128)S(1)}, ...), condition=%wide.region_3.4_spmd.clone, body=%wide.region_2.3_spmd.clone.sunk | while | flops 656122880 | bytes 573567 | solution.py:85
  84.8 2.4 fusion.71
  88.5 2.4 fusion.71
  92.2 2.4 fusion.71
  95.8 2.4 fusion.71
  99.5 2.4 fusion.71
  103.2 2.4 fusion.71
  106.9 2.4 fusion.71
  110.5 2.4 fusion.71
  114.2 2.4 fusion.71
  116.6 36.7 %while.33 = (s32[]{:T(128)}, f32[32,1664]{1,0:T(8,128)S(1)}, f32[10,32,1024]{2,1,0:T(8,128)S(1)}, s32[10]{0:T(128)S(1)}, s32[1664]{0:T(1024)S(1)}, /*index=5*/s32[]{:T(128)}, s32[1]{0:T(128)}, s32[]{:T(128)}) while((s32[]{:T(128)}, f32[32,1664]{1,0:T(8,128)S(1)}, f32[10,32,1024]{2,1,0:T(8,128)S(1)}, s32[10]{0:T(128)S(1)}, ...), condition=%wide.region_1.2_spmd.clone, body=%wide.region_0.1_spmd.clone.sunk | while | flops 656122880 | bytes 573567 | solution.py:85
  121.6 2.4 fusion.68
  125.2 2.4 fusion.68
  128.9 2.4 fusion.68
  132.6 2.4 fusion.68
  136.3 2.4 fusion.68
  154.0 59.3 %while.32 = (s32[]{:T(128)}, f32[10,24,1024]{2,1,0:T(8,128)}, s32[3328]{0:T(1024)S(1)}, s32[10]{0:T(128)S(1)}, f32[24,3328]{1,0:T(8,128)S(1)}, /*index=5*/s32[]{:T(128)}, s32[1]{0:T(128)}) while((s32[]{:T(128)}, f32[10,24,1024]{2,1,0:T(8,128)}, s32[3328]{0:T(1024)S(1)}, s32[10]{0:T(128)S(1)}, f32[24,3328]{1,0:T(8,128)S(1)}, ...), condition=%wide.region_5.6_spmd, body=%wide.region_4.5_spmd.sunk | while | flops 984876032 | bytes 439913 | solution.py:103
  155.3 4.7 %fusion.65 = f32[10,24,1024]{2,1,0:T(8,128)} fusion(f32[10,24,1024]{2,1,0:T(8,128)} %get-tuple-element.346, s32[]{:T(128)} %get-tuple-element.345, f32[24,3328]{1,0:T(8,128)S(1)} %get-tuple-element.356, s32[1024]{0:T(1024)S(1)} %iota_add_fusion.6, s32[3328]{0:T(1024)S(1)} %get-tuple-element.354), kind=kOutput, calls=%fused_computation.5.clone.1 | convolution fusion | flops 984875008 | bytes 435712 | tf_op jit(solution)/shard_map/while/body/eval_jaxpr/dot_general | solution.py:97
  161.2 4.7 %fusion.65 = f32[10,24,1024]{2,1,0:T(8,128)} fusion(f32[10,24,1024]{2,1,0:T(8,128)} %get-tuple-element.346, s32[]{:T(128)} %get-tuple-element.345, f32[24,3328]{1,0:T(8,128)S(1)} %get-tuple-element.356, s32[1024]{0:T(1024)S(1)} %iota_add_fusion.6, s32[3328]{0:T(1024)S(1)} %get-tuple-element.354), kind=kOutput, calls=%fused_computation.5.clone.1 | convolution fusion | flops 984875008 | bytes 435712 | tf_op jit(solution)/shard_map/while/body/eval_jaxpr/dot_general | solution.py:97
  167.2 4.7 %fusion.65 = f32[10,24,1024]{2,1,0:T(8,128)} fusion(f32[10,24,1024]{2,1,0:T(8,128)} %get-tuple-element.346, s32[]{:T(128)} %get-tuple-element.345, f32[24,3328]{1,0:T(8,128)S(1)} %get-tuple-element.356, s32[1024]{0:T(1024)S(1)} %iota_add_fusion.6, s32[3328]{0:T(1024)S(1)} %get-tuple-element.354), kind=kOutput, calls=%fused_computation.5.clone.1 | convolution fusion | flops 984875008 | bytes 435712 | tf_op jit(solution)/shard_map/while/body/eval_jaxpr/dot_general | solution.py:97
  173.1 4.7 %fusion.65 = f32[10,24,1024]{2,1,0:T(8,128)} fusion(f32[10,24,1024]{2,1,0:T(8,128)} %get-tuple-element.346, s32[]{:T(128)} %get-tuple-element.345, f32[24,3328]{1,0:T(8,128)S(1)} %get-tuple-element.356, s32[1024]{0:T(1024)S(1)} %iota_add_fusion.6, s32[3328]{0:T(1024)S(1)} %get-tuple-element.354), kind=kOutput, calls=%fused_computation.5.clone.1 | convolution fusion | flops 984875008 | bytes 435712 | tf_op jit(solution)/shard_map/while/body/eval_jaxpr/dot_general | solution.py:97
  179.0 4.7 %fusion.65 = f32[10,24,1024]{2,1,0:T(8,128)} fusion(f32[10,24,1024]{2,1,0:T(8,128)} %get-tuple-element.346, s32[]{:T(128)} %get-tuple-element.345, f32[24,3328]{1,0:T(8,128)S(1)} %get-tuple-element.356, s32[1024]{0:T(1024)S(1)} %iota_add_fusion.6, s32[3328]{0:T(1024)S(1)} %get-tuple-element.354), kind=kOutput, calls=%fused_computation.5.clone.1 | convolution fusion | flops 984875008 | bytes 435712 | tf_op jit(solution)/shard_map/while/body/eval_jaxpr/dot_general | solution.py:97
  184.9 4.7 %fusion.65 = f32[10,24,1024]{2,1,0:T(8,128)} fusion(f32[10,24,1024]{2,1,0:T(8,128)} %get-tuple-element.346, s32[]{:T(128)} %get-tuple-element.345, f32[24,3328]{1,0:T(8,128)S(1)} %get-tuple-element.356, s32[1024]{0:T(1024)S(1)} %iota_add_fusion.6, s32[3328]{0:T(1024)S(1)} %get-tuple-element.354), kind=kOutput, calls=%fused_computation.5.clone.1 | convolution fusion | flops 984875008 | bytes 435712 | tf_op jit(solution)/shard_map/while/body/eval_jaxpr/dot_general | solution.py:97
  190.9 4.7 %fusion.65 = f32[10,24,1024]{2,1,0:T(8,128)} fusion(f32[10,24,1024]{2,1,0:T(8,128)} %get-tuple-element.346, s32[]{:T(128)} %get-tuple-element.345, f32[24,3328]{1,0:T(8,128)S(1)} %get-tuple-element.356, s32[1024]{0:T(1024)S(1)} %iota_add_fusion.6, s32[3328]{0:T(1024)S(1)} %get-tuple-element.354), kind=kOutput, calls=%fused_computation.5.clone.1 | convolution fusion | flops 984875008 | bytes 435712 | tf_op jit(solution)/shard_map/while/body/eval_jaxpr/dot_general | solution.py:97
  196.8 4.7 %fusion.65 = f32[10,24,1024]{2,1,0:T(8,128)} fusion(f32[10,24,1024]{2,1,0:T(8,128)} %get-tuple-element.346, s32[]{:T(128)} %get-tuple-element.345, f32[24,3328]{1,0:T(8,128)S(1)} %get-tuple-element.356, s32[1024]{0:T(1024)S(1)} %iota_add_fusion.6, s32[3328]{0:T(1024)S(1)} %get-tuple-element.354), kind=kOutput, calls=%fused_computation.5.clone.1 | convolution fusion | flops 984875008 | bytes 435712 | tf_op jit(solution)/shard_map/while/body/eval_jaxpr/dot_general | solution.py:97
  202.7 4.7 %fusion.65 = f32[10,24,1024]{2,1,0:T(8,128)} fusion(f32[10,24,1024]{2,1,0:T(8,128)} %get-tuple-element.346, s32[]{:T(128)} %get-tuple-element.345, f32[24,3328]{1,0:T(8,128)S(1)} %get-tuple-element.356, s32[1024]{0:T(1024)S(1)} %iota_add_fusion.6, s32[3328]{0:T(1024)S(1)} %get-tuple-element.354), kind=kOutput, calls=%fused_computation.5.clone.1 | convolution fusion | flops 984875008 | bytes 435712 | tf_op jit(solution)/shard_map/while/body/eval_jaxpr/dot_general | solution.py:97
  208.7 4.7 %fusion.65 = f32[10,24,1024]{2,1,0:T(8,128)} fusion(f32[10,24,1024]{2,1,0:T(8,128)} %get-tuple-element.346, s32[]{:T(128)} %get-tuple-element.345, f32[24,3328]{1,0:T(8,128)S(1)} %get-tuple-element.356, s32[1024]{0:T(1024)S(1)} %iota_add_fusion.6, s32[3328]{0:T(1024)S(1)} %get-tuple-element.354), kind=kOutput, calls=%fused_computation.5.clone.1 | convolution fusion | flops 984875008 | bytes 435712 | tf_op jit(solution)/shard_map/while/body/eval_jaxpr/dot_general | solution.py:97
  216.6 4.0 %all-to-all-start = ((f32[8,8,3,1280]{3,1,2,0:T(8,128)}), f32[8,8,3,1280]{3,1,2,0:T(8,128)S(1)}, u32[]{:S(2)}, u32[]{:S(2)}) async-start(f32[8,8,3,1280]{3,1,2,0:T(8,128)} %copy.60), calls=%async_computation | async-start | bytes 1966080 | tf_op jit(solution)/shard_map/all_to_all | solution.py:39
  221.5 24.0 %all-to-all-done = f32[8,8,3,1280]{3,1,2,0:T(8,128)S(1)} async-done(((f32[8,8,3,1280]{3,1,2,0:T(8,128)}), f32[8,8,3,1280]{3,1,2,0:T(8,128)S(1)}, u32[]{:S(2)}, u32[]{:S(2)}) %all-to-all-start) | async-done | bytes 983072 | tf_op jit(solution)/shard_map/all_to_all | solution.py:39
  247.1 8.9 %all_to_all.17 = f32[8,1,32]{2,1,0:T(1,128)S(1)} all-to-all(f32[8,1,32]{2,1,0:T(1,128)S(1)} %broadcast_in_dim.14), channel_id=1, replica_groups=mesh['ctg'=32,'br'=8] {'br'}, dimensions={0} | all-to-all | bytes 2048 | tf_op jit(solution)/shard_map/all_to_all | solution.py:45
  256.9 16.7 %all_to_all.18 = f32[32,1,4]{2,1,0:T(1,128)S(1)} all-to-all(f32[32,1,4]{2,1,0:T(1,128)S(1)} %broadcast_in_dim.15), channel_id=1, replica_groups=mesh['ctg'=32,'br'=8] {'ctg'}, dimensions={0} | all-to-all | bytes 1024 | tf_op jit(solution)/shard_map/all_to_all | solution.py:45
  (137 shorter events, 45.0 us)
Async XLA Ops:
  7.2 71.0 %copy-start = (s32[8,1664]{1,0:T(8,128)S(1)}, s32[8,1664]{1,0:T(8,128)}, u32[]{:S(2)}) copy-start(s32[8,1664]{1,0:T(8,128)} %param.29) | copy-start | bytes 159748
  7.2 71.0 %copy-start.9 = (s32[1664]{0:T(1024)S(1)}, s32[1664]{0:T(1024)}, u32[]{:S(2)}) copy-start(s32[1664]{0:T(1024)} %param.28) | copy-start | bytes 19972
  7.2 71.0 %copy-start.10 = (s32[1664]{0:T(1024)S(1)}, s32[1664]{0:T(1024)}, u32[]{:S(2)}) copy-start(s32[1664]{0:T(1024)} %param.27) | copy-start | bytes 19972
  7.2 71.0 %copy-start.2 = (f32[1664]{0:T(1024)S(1)}, f32[1664]{0:T(1024)}, u32[]{:S(2)}) copy-start(f32[1664]{0:T(1024)} %param.31) | copy-start | bytes 19972
  7.2 71.0 %copy-start.8 = (f32[1664]{0:T(1024)S(1)}, f32[1664]{0:T(1024)}, u32[]{:S(2)}) copy-start(f32[1664]{0:T(1024)} %param.32) | copy-start | bytes 19972
  7.2 71.0 %all-gather.3.cloned.1.call-start = ((), (), s32[]{:S(2)}) async-start(), calls=%async_computation.3 | async-start | bytes 1474560 | tf_op jit(solution)/shard_map/all_gather | solution.py:24
  116.6 36.7 %copy-start.6 = (f32[1664]{0:T(1024)S(1)}, f32[1664]{0:T(1024)}, u32[]{:S(2)}) copy-start(f32[1664]{0:T(1024)} %param.30) | copy-start | bytes 19972
  216.6 4.0 %copy-start.7 = (f32[1664]{0:T(1024)S(1)}, f32[1664]{0:T(1024)}, u32[]{:S(2)}) copy-start(f32[1664]{0:T(1024)} %param.33) | copy-start | bytes 19972
  216.6 4.1 %copy-start.3 = (f32[8,1664]{1,0:T(8,128)S(1)}, f32[8,1664]{1,0:T(8,128)}, u32[]{:S(2)}) copy-start(f32[8,1664]{1,0:T(8,128)} %param.34) | copy-start | bytes 159748
  216.6 4.1 %copy-start.4 = (f32[8,1664]{1,0:T(8,128)S(1)}, f32[8,1664]{1,0:T(8,128)}, u32[]{:S(2)}) copy-start(f32[8,1664]{1,0:T(8,128)} %param.35) | copy-start | bytes 159748
  216.6 29.0 %copy-start.5 = (f32[8,1280]{1,0:T(8,128)S(1)}, f32[8,1280]{1,0:T(8,128)}, u32[]{:S(2)}) copy-start(f32[8,1280]{1,0:T(8,128)} %param.26) | copy-start | bytes 122884
  216.6 28.9 %all-to-all-start = ((f32[8,8,3,1280]{3,1,2,0:T(8,128)}), f32[8,8,3,1280]{3,1,2,0:T(8,128)S(1)}, u32[]{:S(2)}, u32[]{:S(2)}) async-start(f32[8,8,3,1280]{3,1,2,0:T(8,128)} %copy.60), calls=%async_computation | async-start | bytes 1966080 | tf_op jit(solution)/shard_map/all_to_all | solution.py:39
  220.7 25.7 %copy-start.1 = (f32[8,2,1280]{2,1,0:T(2,128)S(1)}, f32[8,2,1280]{2,1,0:T(2,128)}, u32[]{:S(2)}) copy-start(f32[8,2,1280]{2,1,0:T(2,128)} %param.25) | copy-start | bytes 245764
Sparse Core Ops, SparseCore 0:
  9.9 38.6 all-gather.2
where the time goes:
time: 283 us; the launch traced here: 281 us
  matrix products  94.7 us (33%)
  blocking collectives  92.8 us (33%)
  local copies, waits for them, and re-layouts  24.9 us (9%)
  waiting for transfers between devices  24.1 us (9%)
  loops' own time  20.3 us (7%)
  between operations  14.4 us (5%)
  other arithmetic  5.73 us (2%)
  starting transfers between devices  4.05 us (1%)
    all_gather x1, blocking collectives, turned_gather(): whole = lax.all_gather(both, axis, axis=0, tiled=True)  67.2 us
    dot_general x20, matrix products, add_block(): jnp.dot(segment, onehot, precision=lax.Precision.HIGHEST, preferred_eleme...  47.9 us
    dot_general x10, matrix products, one_block(): jnp.dot(values, onehot, precision=lax.Precision.HIGHEST, preferred_elemen...  46.8 us
    all_to_all x2, blocking collectives, sent_to_all(): return lax.all_to_all(copies, axis, split_axis=0, concat_axis=0, tiled=True)  25.6 us
    all_to_all x1, waiting for transfers between devices, summed_on_arrival(): lax.all_to_all(in_blocks(array, dim, peers), axis, 0, 0, tiled=True)  24 us
    dynamic_slice x30, local copies, waits for them, and re-layouts, select_cols(): result, _ = lax.scan(add_block, start_zero, (tiles, numbers))  17.6 us
    another operation x2, loops' own time, select_cols(): result, _ = lax.scan(add_block, start_zero, (tiles, numbers))  13.7 us
    another operation x1, loops' own time, spread_rows(): _, pieces = lax.scan(one_block, jnp.int32(0), numbers)  6.61 us
  transfers between devices with their start and end apart: 2, of which 1 were waited for; matrix products, arithmetic and copies ran while one was open for 1% of the time, Pallas kernels for 0%

commit v1 on v0

--- a/solution.py
+++ b/solution.py
@@ -9,7 +9,8 @@
     turned = [jnp.moveaxis(a, dim, 0) for a, dim in zip(arrays, dims)]
     widths = [t[0].size for t in turned]
     both = jnp.concatenate([t.reshape(-1, w) for t, w in zip(turned, widths)], axis=1)
-    whole = lax.all_gather(both, axis, axis=0, tiled=True)
+    sent = jnp.stack([both] * lax.axis_size(axis))
+    whole = jnp.concatenate(lax.all_to_all(sent, axis, 0, 0), axis=0)
     pieces = jnp.split(whole, [sum(widths[:k]) for k in range(1, len(widths))], axis=1)
     return tuple(
         (

time: 283 us -> 257 us (0.908)
  blocking collectives: 92.8 us -> 27.8 us
  waiting for transfers between devices: 24.1 us -> 47.5 us
  starting transfers between devices: 4.05 us -> 19.7 us
    all_gather x1 -> x0, blocking collectives: 67.2 us -> none  [turned_gather(): whole = lax.all_gather(both, axis, axis=0, tiled=True)]
    all_to_all x0 -> x1, waiting for transfers between devices: none -> 18.3 us  [turned_gather(): whole = jnp.concatenate(lax.all_to_all(sent, axis, 0, 0), axis=0)]
    all_to_all x0 -> x1, starting transfers between devices: none -> 15.6 us  [turned_gather(): whole = jnp.concatenate(lax.all_to_all(sent, axis, 0, 0), axis=0)]
    all_gather x1, waiting for transfers between devices: 0.02 us -> 5.84 us  [in_one_piece(): lax.all_gather(both, axis, axis=dim, tiled=True)]
  transfers between devices with their start and end apart: 2 -> 3, of which waited for: 1 -> 3; matrix products, arithmetic and copies ran while one was open for 1% -> 1% of each run, Pallas kernels for 0% -> 0%
where the time goes in v1:
time: 257 us; the launch traced here: 256 us
  matrix products  94.8 us (37%)
  waiting for transfers between devices  47.5 us (18%)
  blocking collectives  27.8 us (11%)
  local copies, waits for them, and re-layouts  25.7 us (10%)
  loops' own time  20.3 us (8%)
  starting transfers between devices  19.7 us (8%)
  between operations  14.4 us (6%)
  other arithmetic  5.66 us (2%)
    dot_general x20, matrix products, add_block(): jnp.dot(segment, onehot, precision=lax.Precision.HIGHEST, preferred_eleme...  47.9 us
    dot_general x10, matrix products, one_block(): jnp.dot(values, onehot, precision=lax.Precision.HIGHEST, preferred_elemen...  46.9 us
    all_to_all x2, blocking collectives, sent_to_all(): return lax.all_to_all(copies, axis, split_axis=0, concat_axis=0, tiled=True)  27.8 us
    all_to_all x1, waiting for transfers between devices, summed_on_arrival(): lax.all_to_all(in_blocks(array, dim, peers), axis, 0, 0, tiled=True)  23.4 us
    all_to_all x1, waiting for transfers between devices, turned_gather(): whole = jnp.concatenate(lax.all_to_all(sent, axis, 0, 0), axis=0)  18.3 us
    dynamic_slice x30, local copies, waits for them, and re-layouts, select_cols(): result, _ = lax.scan(add_block, start_zero, (tiles, numbers))  17.6 us
    all_to_all x1, starting transfers between devices, turned_gather(): whole = jnp.concatenate(lax.all_to_all(sent, axis, 0, 0), axis=0)  15.6 us
    another operation x2, loops' own time, select_cols(): result, _ = lax.scan(add_block, start_zero, (tiles, numbers))  13.7 us
  transfers between devices with their start and end apart: 3, of which 3 were waited for; matrix products, arithmetic and copies ran while one was open for 1% of the time, Pallas kernels for 0%

profile of v1, /device:TPU:1, one launch (start us, length us, event | category | flops | bytes accessed | tf_op | source)
XLA Modules:
  0.0 255.8 jit_solution(12255671352523223641)
XLA Ops:
  11.2 15.6 %all-to-all-start = ((f32[256,40,2]{1,2,0:T(2,128)}), f32[256,40,2]{1,2,0:T(2,128)S(1)}, u32[]{:S(2)}, u32[]{:S(2)}) async-start(f32[256,40,2]{1,2,0:T(2,128)} %stack.28), calls=%async_computation | async-start | bytes 524288 | tf_op jit(solution)/shard_map/all_to_all | solution.py:13
  27.0 18.3 %all-to-all-done = f32[256,40,2]{1,2,0:T(2,128)S(1)} async-done(((f32[256,40,2]{1,2,0:T(2,128)}), f32[256,40,2]{1,2,0:T(2,128)S(1)}, u32[]{:S(2)}, u32[]{:S(2)}) %all-to-all-start) | async-done | bytes 81952 | tf_op jit(solution)/shard_map/all_to_all | solution.py:13
  45.7 5.8 %all-gather.2.cloned.1.call-done = f32[16,2,10240]{2,0,1:T(8,128)} async-done(((f32[16,2,1280]{2,0,1:T(8,128)}), f32[16,2,10240]{2,0,1:T(8,128)}) %all-gather.2.cloned.1.call-update) | async-done | bytes 1310736 | tf_op jit(solution)/shard_map/all_gather | solution.py:25
  53.1 36.7 %while.34 = (s32[]{:T(128)}, f32[32,1664]{1,0:T(8,128)S(1)}, f32[10,32,1024]{2,1,0:T(8,128)S(1)}, s32[10]{0:T(128)S(1)}, s32[1664]{0:T(1024)S(1)}, /*index=5*/s32[]{:T(128)}, s32[1]{0:T(128)}, s32[]{:T(128)}) while((s32[]{:T(128)}, f32[32,1664]{1,0:T(8,128)S(1)}, f32[10,32,1024]{2,1,0:T(8,128)S(1)}, s32[10]{0:T(128)S(1)}, ...), condition=%wide.region_3.4_spmd.clone, body=%wide.region_2.3_spmd.clone.sunk | while | flops 656122880 | bytes 573567 | solution.py:86
  54.4 2.4 fusion.71
  58.0 2.4 fusion.71
  61.7 2.4 fusion.71
  65.4 2.4 fusion.71
  69.1 2.4 fusion.71
  72.7 2.4 fusion.71
  76.4 2.4 fusion.71
  80.1 2.4 fusion.71
  83.7 2.4 fusion.71
  87.4 2.4 fusion.71
  89.8 36.7 %while.33 = (s32[]{:T(128)}, f32[32,1664]{1,0:T(8,128)S(1)}, f32[10,32,1024]{2,1,0:T(8,128)S(1)}, s32[10]{0:T(128)S(1)}, s32[1664]{0:T(1024)S(1)}, /*index=5*/s32[]{:T(128)}, s32[1]{0:T(128)}, s32[]{:T(128)}) while((s32[]{:T(128)}, f32[32,1664]{1,0:T(8,128)S(1)}, f32[10,32,1024]{2,1,0:T(8,128)S(1)}, s32[10]{0:T(128)S(1)}, ...), condition=%wide.region_1.2_spmd.clone, body=%wide.region_0.1_spmd.clone.sunk | while | flops 656122880 | bytes 573567 | solution.py:86
  94.8 2.4 fusion.68
  98.5 2.4 fusion.68
  127.3 59.3 %while.32 = (s32[]{:T(128)}, f32[10,24,1024]{2,1,0:T(8,128)}, s32[3328]{0:T(1024)S(1)}, s32[10]{0:T(128)S(1)}, f32[24,3328]{1,0:T(8,128)S(1)}, /*index=5*/s32[]{:T(128)}, s32[1]{0:T(128)}) while((s32[]{:T(128)}, f32[10,24,1024]{2,1,0:T(8,128)}, s32[3328]{0:T(1024)S(1)}, s32[10]{0:T(128)S(1)}, f32[24,3328]{1,0:T(8,128)S(1)}, ...), condition=%wide.region_5.6_spmd, body=%wide.region_4.5_spmd.sunk | while | flops 984876032 | bytes 439913 | solution.py:104
  128.5 4.7 %fusion.65 = f32[10,24,1024]{2,1,0:T(8,128)} fusion(f32[10,24,1024]{2,1,0:T(8,128)} %get-tuple-element.346, s32[]{:T(128)} %get-tuple-element.345, f32[24,3328]{1,0:T(8,128)S(1)} %get-tuple-element.356, s32[1024]{0:T(1024)S(1)} %iota_add_fusion.6, s32[3328]{0:T(1024)S(1)} %get-tuple-element.354), kind=kOutput, calls=%fused_computation.5.clone.1 | convolution fusion | flops 984875008 | bytes 435712 | tf_op jit(solution)/shard_map/while/body/eval_jaxpr/dot_general | solution.py:98
  134.5 4.7 %fusion.65 = f32[10,24,1024]{2,1,0:T(8,128)} fusion(f32[10,24,1024]{2,1,0:T(8,128)} %get-tuple-element.346, s32[]{:T(128)} %get-tuple-element.345, f32[24,3328]{1,0:T(8,128)S(1)} %get-tuple-element.356, s32[1024]{0:T(1024)S(1)} %iota_add_fusion.6, s32[3328]{0:T(1024)S(1)} %get-tuple-element.354), kind=kOutput, calls=%fused_computation.5.clone.1 | convolution fusion | flops 984875008 | bytes 435712 | tf_op jit(solution)/shard_map/while/body/eval_jaxpr/dot_general | solution.py:98
  140.4 4.7 %fusion.65 = f32[10,24,1024]{2,1,0:T(8,128)} fusion(f32[10,24,1024]{2,1,0:T(8,128)} %get-tuple-element.346, s32[]{:T(128)} %get-tuple-element.345, f32[24,3328]{1,0:T(8,128)S(1)} %get-tuple-element.356, s32[1024]{0:T(1024)S(1)} %iota_add_fusion.6, s32[3328]{0:T(1024)S(1)} %get-tuple-element.354), kind=kOutput, calls=%fused_computation.5.clone.1 | convolution fusion | flops 984875008 | bytes 435712 | tf_op jit(solution)/shard_map/while/body/eval_jaxpr/dot_general | solution.py:98
  146.3 4.7 %fusion.65 = f32[10,24,1024]{2,1,0:T(8,128)} fusion(f32[10,24,1024]{2,1,0:T(8,128)} %get-tuple-element.346, s32[]{:T(128)} %get-tuple-element.345, f32[24,3328]{1,0:T(8,128)S(1)} %get-tuple-element.356, s32[1024]{0:T(1024)S(1)} %iota_add_fusion.6, s32[3328]{0:T(1024)S(1)} %get-tuple-element.354), kind=kOutput, calls=%fused_computation.5.clone.1 | convolution fusion | flops 984875008 | bytes 435712 | tf_op jit(solution)/shard_map/while/body/eval_jaxpr/dot_general | solution.py:98
  152.2 4.7 %fusion.65 = f32[10,24,1024]{2,1,0:T(8,128)} fusion(f32[10,24,1024]{2,1,0:T(8,128)} %get-tuple-element.346, s32[]{:T(128)} %get-tuple-element.345, f32[24,3328]{1,0:T(8,128)S(1)} %get-tuple-element.356, s32[1024]{0:T(1024)S(1)} %iota_add_fusion.6, s32[3328]{0:T(1024)S(1)} %get-tuple-element.354), kind=kOutput, calls=%fused_computation.5.clone.1 | convolution fusion | flops 984875008 | bytes 435712 | tf_op jit(solution)/shard_map/while/body/eval_jaxpr/dot_general | solution.py:98
  158.2 4.7 %fusion.65 = f32[10,24,1024]{2,1,0:T(8,128)} fusion(f32[10,24,1024]{2,1,0:T(8,128)} %get-tuple-element.346, s32[]{:T(128)} %get-tuple-element.345, f32[24,3328]{1,0:T(8,128)S(1)} %get-tuple-element.356, s32[1024]{0:T(1024)S(1)} %iota_add_fusion.6, s32[3328]{0:T(1024)S(1)} %get-tuple-element.354), kind=kOutput, calls=%fused_computation.5.clone.1 | convolution fusion | flops 984875008 | bytes 435712 | tf_op jit(solution)/shard_map/while/body/eval_jaxpr/dot_general | solution.py:98
  164.1 4.7 %fusion.65 = f32[10,24,1024]{2,1,0:T(8,128)} fusion(f32[10,24,1024]{2,1,0:T(8,128)} %get-tuple-element.346, s32[]{:T(128)} %get-tuple-element.345, f32[24,3328]{1,0:T(8,128)S(1)} %get-tuple-element.356, s32[1024]{0:T(1024)S(1)} %iota_add_fusion.6, s32[3328]{0:T(1024)S(1)} %get-tuple-element.354), kind=kOutput, calls=%fused_computation.5.clone.1 | convolution fusion | flops 984875008 | bytes 435712 | tf_op jit(solution)/shard_map/while/body/eval_jaxpr/dot_general | solution.py:98
  170.0 4.7 %fusion.65 = f32[10,24,1024]{2,1,0:T(8,128)} fusion(f32[10,24,1024]{2,1,0:T(8,128)} %get-tuple-element.346, s32[]{:T(128)} %get-tuple-element.345, f32[24,3328]{1,0:T(8,128)S(1)} %get-tuple-element.356, s32[1024]{0:T(1024)S(1)} %iota_add_fusion.6, s32[3328]{0:T(1024)S(1)} %get-tuple-element.354), kind=kOutput, calls=%fused_computation.5.clone.1 | convolution fusion | flops 984875008 | bytes 435712 | tf_op jit(solution)/shard_map/while/body/eval_jaxpr/dot_general | solution.py:98
  176.0 4.7 %fusion.65 = f32[10,24,1024]{2,1,0:T(8,128)} fusion(f32[10,24,1024]{2,1,0:T(8,128)} %get-tuple-element.346, s32[]{:T(128)} %get-tuple-element.345, f32[24,3328]{1,0:T(8,128)S(1)} %get-tuple-element.356, s32[1024]{0:T(1024)S(1)} %iota_add_fusion.6, s32[3328]{0:T(1024)S(1)} %get-tuple-element.354), kind=kOutput, calls=%fused_computation.5.clone.1 | convolution fusion | flops 984875008 | bytes 435712 | tf_op jit(solution)/shard_map/while/body/eval_jaxpr/dot_general | solution.py:98
  181.9 4.7 %fusion.65 = f32[10,24,1024]{2,1,0:T(8,128)} fusion(f32[10,24,1024]{2,1,0:T(8,128)} %get-tuple-element.346, s32[]{:T(128)} %get-tuple-element.345, f32[24,3328]{1,0:T(8,128)S(1)} %get-tuple-element.356, s32[1024]{0:T(1024)S(1)} %iota_add_fusion.6, s32[3328]{0:T(1024)S(1)} %get-tuple-element.354), kind=kOutput, calls=%fused_computation.5.clone.1 | convolution fusion | flops 984875008 | bytes 435712 | tf_op jit(solution)/shard_map/while/body/eval_jaxpr/dot_general | solution.py:98
  189.9 4.0 %all-to-all-start.1 = ((f32[8,8,3,1280]{3,1,2,0:T(8,128)}), f32[8,8,3,1280]{3,1,2,0:T(8,128)S(1)}, u32[]{:S(2)}, u32[]{:S(2)}) async-start(f32[8,8,3,1280]{3,1,2,0:T(8,128)} %copy.59), calls=%async_computation.1 | async-start | bytes 1966080 | tf_op jit(solution)/shard_map/all_to_all | solution.py:40
  194.8 23.4 %all-to-all-done.1 = f32[8,8,3,1280]{3,1,2,0:T(8,128)S(1)} async-done(((f32[8,8,3,1280]{3,1,2,0:T(8,128)}), f32[8,8,3,1280]{3,1,2,0:T(8,128)S(1)}, u32[]{:S(2)}, u32[]{:S(2)}) %all-to-all-start.1) | async-done | bytes 983072 | tf_op jit(solution)/shard_map/all_to_all | solution.py:40
  219.8 8.9 %all_to_all.22 = f32[8,1,32]{2,1,0:T(1,128)S(1)} all-to-all(f32[8,1,32]{2,1,0:T(1,128)S(1)} %broadcast_in_dim.14), channel_id=1, replica_groups=mesh['ctg'=32,'br'=8] {'br'}, dimensions={0} | all-to-all | bytes 2048 | tf_op jit(solution)/shard_map/all_to_all | solution.py:46
  229.5 18.9 %all_to_all.23 = f32[32,1,4]{2,1,0:T(1,128)S(1)} all-to-all(f32[32,1,4]{2,1,0:T(1,128)S(1)} %broadcast_in_dim.15), channel_id=1, replica_groups=mesh['ctg'=32,'br'=8] {'ctg'}, dimensions={0} | all-to-all | bytes 1024 | tf_op jit(solution)/shard_map/all_to_all | solution.py:46
  (139 shorter events, 50.5 us)
Async XLA Ops:
  7.2 19.7 %copy-start.2 = (f32[1664]{0:T(1024)S(1)}, f32[1664]{0:T(1024)}, u32[]{:S(2)}) copy-start(f32[1664]{0:T(1024)} %param.31) | copy-start | bytes 19972
  7.2 19.7 %copy-start.8 = (f32[1664]{0:T(1024)S(1)}, f32[1664]{0:T(1024)}, u32[]{:S(2)}) copy-start(f32[1664]{0:T(1024)} %param.32) | copy-start | bytes 19972
  7.2 19.7 %copy-start = (s32[8,1664]{1,0:T(8,128)S(1)}, s32[8,1664]{1,0:T(8,128)}, u32[]{:S(2)}) copy-start(s32[8,1664]{1,0:T(8,128)} %param.29) | copy-start | bytes 159748
  7.2 19.7 %copy-start.9 = (s32[1664]{0:T(1024)S(1)}, s32[1664]{0:T(1024)}, u32[]{:S(2)}) copy-start(s32[1664]{0:T(1024)} %param.28) | copy-start | bytes 19972
  7.2 19.7 %copy-start.10 = (s32[1664]{0:T(1024)S(1)}, s32[1664]{0:T(1024)}, u32[]{:S(2)}) copy-start(s32[1664]{0:T(1024)} %param.27) | copy-start | bytes 19972
  7.2 44.3 %all-gather.2.cloned.1.call-start = ((), (), s32[]{:S(2)}) async-start(), calls=%async_computation.4 | async-start | bytes 1474560 | tf_op jit(solution)/shard_map/all_gather | solution.py:25
  11.2 34.0 %all-to-all-start = ((f32[256,40,2]{1,2,0:T(2,128)}), f32[256,40,2]{1,2,0:T(2,128)S(1)}, u32[]{:S(2)}, u32[]{:S(2)}) async-start(f32[256,40,2]{1,2,0:T(2,128)} %stack.28), calls=%async_computation | async-start | bytes 524288 | tf_op jit(solution)/shard_map/all_to_all | solution.py:13
  89.8 36.7 %copy-start.6 = (f32[1664]{0:T(1024)S(1)}, f32[1664]{0:T(1024)}, u32[]{:S(2)}) copy-start(f32[1664]{0:T(1024)} %param.30) | copy-start | bytes 19972
  189.9 4.0 %copy-start.7 = (f32[1664]{0:T(1024)S(1)}, f32[1664]{0:T(1024)}, u32[]{:S(2)}) copy-start(f32[1664]{0:T(1024)} %param.33) | copy-start | bytes 19972
  189.9 4.1 %copy-start.3 = (f32[8,1664]{1,0:T(8,128)S(1)}, f32[8,1664]{1,0:T(8,128)}, u32[]{:S(2)}) copy-start(f32[8,1664]{1,0:T(8,128)} %param.34) | copy-start | bytes 159748
  189.9 4.1 %copy-start.4 = (f32[8,1664]{1,0:T(8,128)S(1)}, f32[8,1664]{1,0:T(8,128)}, u32[]{:S(2)}) copy-start(f32[8,1664]{1,0:T(8,128)} %param.35) | copy-start | bytes 159748
  189.9 28.3 %copy-start.5 = (f32[8,1280]{1,0:T(8,128)S(1)}, f32[8,1280]{1,0:T(8,128)}, u32[]{:S(2)}) copy-start(f32[8,1280]{1,0:T(8,128)} %param.26) | copy-start | bytes 122884
  189.9 28.2 %all-to-all-start.1 = ((f32[8,8,3,1280]{3,1,2,0:T(8,128)}), f32[8,8,3,1280]{3,1,2,0:T(8,128)S(1)}, u32[]{:S(2)}, u32[]{:S(2)}) async-start(f32[8,8,3,1280]{3,1,2,0:T(8,128)} %copy.59), calls=%async_computation.1 | async-start | bytes 1966080 | tf_op jit(solution)/shard_map/all_to_all | solution.py:40
  193.9 25.0 %copy-start.1 = (f32[8,2,1280]{2,1,0:T(2,128)S(1)}, f32[8,2,1280]{2,1,0:T(2,128)}, u32[]{:S(2)}) copy-start(f32[8,2,1280]{2,1,0:T(2,128)} %param.25) | copy-start | bytes 245764
Sparse Core Ops, SparseCore 0:
  9.9 41.6 all-gather.1
